TPU v7x, 32 devices: a whole 2x2x4 slice. The times are simulated.
32 devices in a mesh: gz: 2 (over core), pa: 16 (over z, y, x).
Axes of the slice: x: 2, y: 2, z: 4, core: 2. Of those that a mesh axis runs over, the one named last changes fastest.
Arguments:
- velocity: float32 [3, 2, 2, 512, 1024], P(None, 'gz', None, 'pa'), may hold values from -3 to 3
- mode_mask: int32 [512, 1024], P('pa'), may hold values from 0 to 1, as said below
Outputs:
- velocity_next: float32 [3, 2, 2, 512, 1024], P(None, 'gz', None, 'pa')
- divergence: float32 [2, 2, 512, 1024], P('gz', None, 'pa')
Inputs may be any that keep to these rules, and one draw needn't show every extreme that they name: mode_mask is 1 exactly where |s(m)| <= A and n <= B, for one A from 256 to 340 and one B from 256 to 340 in each draw, and 0 elsewhere.
All inputs are finite; a program needn't handle non-finite values.
Results may differ from a plain program's by a relative error of at most 0.00005.
Values sent between devices are 32-bit elements; how exact they have to be, the bound alone decides.
No kernel may reach another device: no remote copies, remote signals or barrier semaphores. Data moves between devices by JAX's collectives and lax.ppermute only.
A program may use at most 64 MiB of HBM per device.

v0:
```python
import functools
import math

import jax
import jax.numpy as jnp
import ml_dtypes
import numpy as np
from jax import lax
from jax.experimental import pallas as pl
from jax.experimental.pallas import tpu as pltpu
from jax.sharding import PartitionSpec as P

time_step = 0.2
viscosity = 0.25
LANES = 128
HALF = LANES // 2
ROWS = 8


def halves(table):
    high = table.astype(np.float32).astype(ml_dtypes.bfloat16)
    low = (table - high.astype(np.float64)).astype(np.float32).astype(ml_dtypes.bfloat16)
    return np.stack([high, low])


def wheel(rows, cols, period):
    angle = 2.0 * np.pi / period * (np.outer(rows, cols) % period)
    return np.cos(angle), np.sin(angle)


@functools.lru_cache(maxsize=None)
def tables(ncols, half, lines):
    radix = ncols // LANES
    lane = np.arange(LANES)
    scale = 1.0 / math.sqrt(ncols)
    cos, sin = wheel(lane, lane, LANES)
    forward = np.zeros((2 * LANES, 2 * LANES))
    for part in range(LANES // lines):
        x2 = np.arange(part * lines, (part + 1) * lines)
        at = part * 2 * lines
        forward[:LANES, at : at + lines] = cos[:, x2]
        forward[LANES:, at : at + lines] = -sin[:, x2]
        forward[:LANES, at + lines : at + 2 * lines] = sin[:, x2]
        forward[LANES:, at + lines : at + 2 * lines] = cos[:, x2]
    backward = forward.T
    turn_cos, turn_sin = wheel(np.arange(radix), lane, ncols)
    turns = np.concatenate([turn_cos, turn_sin]).astype(np.float32)
    quarter = half // 2
    nrows = 2 * half
    b = np.arange(quarter)
    yscale = 1.0 / math.sqrt(nrows)
    ycos, ysin = wheel(b, b, quarter)
    to_grid = 2.0 * yscale * np.concatenate([ycos, -ysin], 1)
    from_grid = yscale * np.concatenate([ycos, -ysin], 0)
    column = np.zeros((quarter, LANES))
    for y1 in range(1, 4):
        c, s = wheel(b, np.array([y1]), nrows)
        column[:, 2 * y1] = c[:, 0]
        column[:, 2 * y1 + 1] = s[:, 0]
    modes = np.arange(ncols)
    signed = np.where(modes < ncols // 2, modes, modes - ncols).astype(np.float32)
    wave = np.broadcast_to(np.float32(2.0 * math.pi / ncols) * signed, (ROWS, ncols))
    return dict(
        forward=halves(forward * scale),
        backward=halves(backward * scale),
        turns=turns,
        to_grid=halves(to_grid),
        from_grid=halves(from_grid),
        column=column.astype(np.float32),
        wave=np.ascontiguousarray(wave),
    )


def split(value):
    high = value.astype(jnp.bfloat16)
    low = (value - high.astype(jnp.float32)).astype(jnp.bfloat16)
    return high, low


def product(a_high, a_low, b_high, b_low):
    dot = functools.partial(jnp.dot, preferred_element_type=jnp.float32)
    return dot(a_high, b_low) + dot(a_low, b_high) + dot(a_high, b_high)


def butterfly(terms, sign):
    count = len(terms)
    if count == 1:
        return terms
    even = butterfly(terms[0::2], sign)
    odd = butterfly(terms[1::2], sign)
    first, second = [], []
    for k in range(count // 2):
        real, imag = odd[k]
        if k == 0:
            pass
        elif 4 * k == count:
            real, imag = -sign * imag, sign * real
        elif 8 * k == count:
            root = math.sqrt(0.5)
            real, imag = root * (real - sign * imag), root * (imag + sign * real)
        elif 8 * k == 3 * count:
            root = math.sqrt(0.5)
            real, imag = -root * (real + sign * imag), root * (sign * real - imag)
        else:
            c = math.cos(2.0 * math.pi * k / count)
            s = sign * math.sin(2.0 * math.pi * k / count)
            real, imag = c * real - s * imag, s * real + c * imag
        first.append((even[k][0] + real, even[k][1] + imag))
        second.append((even[k][0] - real, even[k][1] - imag))
    return first + second


def x_forward_kernel(vel_ref, wave_ref, turn_ref, mat_ref, out_ref, mid_ref):
    kyl, ncols = vel_ref.shape[2:]
    radix = ncols // LANES

    def chunk(c, carry):
        base = pl.multiple_of(c * ROWS, ROWS)
        rows = pl.ds(base, ROWS)

        def emit(field, terms):
            for x1, (real, imag) in enumerate(butterfly(terms, 1.0)):
                if x1:
                    cos = turn_ref[x1 : x1 + 1, :]
                    sin = turn_ref[radix + x1 : radix + x1 + 1, :]
                    real, imag = real * cos - imag * sin, real * sin + imag * cos
                at = pl.ds(pl.multiple_of(field * kyl + base, ROWS), ROWS)
                mid_ref[x1, at, 0:LANES] = real
                mid_ref[x1, at, LANES : 2 * LANES] = imag

        def load(field):
            cols = [slice(a * LANES, (a + 1) * LANES) for a in range(radix)]
            return [(vel_ref[field, 0, rows, s], vel_ref[field, 1, rows, s]) for s in cols]

        def slope(terms):
            waves = [wave_ref[:, a * LANES : (a + 1) * LANES] for a in range(radix)]
            return [(-k * imag, k * real) for k, (real, imag) in zip(waves, terms)]

        emit(0, load(0))
        emit(1, load(1))
        emit(2, load(2))
        emit(3, slope(load(2)))
        emit(4, slope(load(1)))
        return carry

    lax.fori_loop(0, kyl // ROWS, chunk, 0)
    for x1 in range(radix):
        high, low = split(mid_ref[x1])
        lines = product(high, low, mat_ref[0], mat_ref[1])
        out_ref[2 * x1] = lines[:, :LANES]
        out_ref[2 * x1 + 1] = lines[:, LANES:]


def grid_kernel(recv_ref, wall_ref, to_ref, from_ref, column_ref, out_ref, high_ref, low_ref, back_high, back_low):
    groups = recv_ref.shape[0]
    kyl = recv_ref.shape[1] // 5
    quarter = groups * kyl // 2
    block = 32
    each = block // kyl
    gap = groups // 2
    ky_step = 2.0 * math.pi / (4 * quarter)
    left = lax.broadcasted_iota(jnp.int32, (block, LANES), 1) < HALF
    swap = lambda value: pltpu.roll(value, HALF, 1)

    def fields(first, row):
        sources = pl.ds(first, each)
        load = lambda ref, f: ref[sources, f * kyl : (f + 1) * kyl, :].reshape(block, LANES)
        index = row + lax.broadcasted_iota(jnp.int32, (block, LANES), 0)
        ky = index.astype(jnp.float32) * ky_step
        weight = jnp.where(index == 0, 0.5, 1.0)
        ky_signed = jnp.where(left, -ky, ky)
        u, v, w, dw, dv = [load(recv_ref, f) for f in range(5)]
        du_dz, dv_dz = load(wall_ref, 0), load(wall_ref, 1)
        omega_x = ky_signed * swap(w) - dv_dz
        omega_y = du_dz - dw
        omega_z = dv - ky_signed * swap(u)
        result = []
        for one, two in ((u, v), (omega_x, omega_y), (w, omega_z)):
            one = one * weight
            two = two * weight
            result.append((jnp.where(left, one, swap(two)), jnp.where(left, swap(one), two)))
        return result

    def column(rows, k):
        return jnp.broadcast_to(column_ref[rows, k : k + 1], (block, LANES))

    def load_block(c, carry):
        base = pl.multiple_of(c * block, block)
        rows = pl.ds(base, block)
        near = fields(c * each, base)
        far = fields(c * each + gap, base + quarter)
        for pair in range(3):
            a_re, a_im = near[pair]
            b_re, b_im = far[pair]
            sums = (
                (a_re + b_re, a_im + b_im),
                (a_re - b_im, a_im + b_re),
                (a_re - b_re, a_im - b_im),
                (a_re + b_im, a_im - b_re),
            )
            for y1, (real, imag) in enumerate(sums):
                if y1:
                    cos = column(rows, 2 * y1)
                    sin = column(rows, 2 * y1 + 1)
                    real, imag = real * cos - imag * sin, real * sin + imag * cos
                at = slice((3 * y1 + pair) * LANES, (3 * y1 + pair + 1) * LANES)
                lower = pl.ds(pl.multiple_of(quarter + base, block), block)
                high_ref[rows, at], low_ref[rows, at] = split(real)
                high_ref[lower, at], low_ref[lower, at] = split(imag)
        return carry

    lax.fori_loop(0, quarter // block, load_block, 0)

    wide = lax.broadcasted_iota(jnp.int32, (quarter, LANES), 1) < HALF
    kept = None
    for y1 in range(4):
        at = slice(3 * y1 * LANES, 3 * (y1 + 1) * LANES)
        grid = product(to_ref[0], to_ref[1], high_ref[:, at], low_ref[:, at])
        uv = grid[:, :LANES]
        xy = grid[:, LANES : 2 * LANES]
        wz = grid[:, 2 * LANES :]
        zw = swap(wz)
        h_yx = jnp.where(wide, wz, zw) * xy - jnp.where(wide, zw, wz) * uv
        spin = uv * swap(xy)
        h_z = spin - swap(spin)
        slot = slice(y1 * LANES, (y1 + 1) * LANES)
        back_high[:, slot], back_low[:, slot] = split(h_yx)
        if y1 % 2 == 0:
            kept = h_z
        else:
            slot = slice((4 + y1 // 2) * LANES, (5 + y1 // 2) * LANES)
            back_high[:, slot], back_low[:, slot] = split(jnp.where(wide, kept, -h_z))

    freq = product(from_ref[0], from_ref[1], back_high[...], back_low[...])

    column_all = lambda k: jnp.broadcast_to(column_ref[:, k : k + 1], (quarter, LANES))

    def piece(slot, cos, sin):
        real = freq[:quarter, slot * LANES : (slot + 1) * LANES]
        imag = freq[quarter:, slot * LANES : (slot + 1) * LANES]
        if cos is None:
            return real, imag
        return real * cos + imag * sin, imag * cos - real * sin

    turn = [(None, None)] + [(column_all(2 * y1), column_all(2 * y1 + 1)) for y1 in range(1, 4)]
    one = jnp.ones((quarter, LANES), jnp.float32)
    zero = jnp.zeros((quarter, LANES), jnp.float32)
    q0, q1, q2, q3 = [piece(y1, *turn[y1]) for y1 in range(4)]
    z01 = piece(4, jnp.where(wide, one, turn[1][0]), jnp.where(wide, zero, turn[1][1]))
    z23 = piece(5, jnp.where(wide, turn[2][0], turn[3][0]), jnp.where(wide, turn[2][1], turn[3][1]))
    near_re = q0[0] + q1[0] + q2[0] + q3[0]
    near_im = q0[1] + q1[1] + q2[1] + q3[1]
    far_re = q0[0] + q1[1] - q2[0] - q3[1]
    far_im = q0[1] - q1[0] - q2[1] + q3[0]
    v_re, v_im = z01[0] + z23[0], z01[1] + z23[1]
    z_near = jnp.where(wide, v_re + swap(v_re), v_im + swap(v_im))
    d_re, d_im = z01[0] - z23[0], z01[1] - z23[1]
    z_far = jnp.where(wide, d_re + swap(d_im), swap(d_im) - d_re)

    def store(first, field, value):
        for s in range(gap):
            out_ref[first + s, field * kyl : (field + 1) * kyl, :] = value[s * kyl : (s + 1) * kyl]

    for first, real, imag, h_z in ((0, near_re, near_im, z_near), (gap, far_re, far_im, z_far)):
        store(first, 0, -jnp.where(wide, swap(real), imag))
        store(first, 1, jnp.where(wide, real, swap(imag)))
        store(first, 2, h_z)


def x_backward_kernel(recv_ref, vel_ref, side_ref, mask_ref, ky_ref, wave_ref, turn_ref, mat_ref, next_ref, div_ref, w_ref, mid_ref):
    kyl, ncols = vel_ref.shape[2:]
    radix = ncols // LANES
    for x1 in range(radix):
        high, low = split(jnp.concatenate([recv_ref[2 * x1], recv_ref[2 * x1 + 1]], axis=1))
        freq = product(high, low, mat_ref[0], mat_ref[1])
        real = freq[:, :LANES]
        imag = freq[:, LANES:]
        if x1:
            cos = turn_ref[x1 : x1 + 1, :]
            sin = turn_ref[radix + x1 : radix + x1 + 1, :]
            real, imag = real * cos + imag * sin, imag * cos - real * sin
        mid_ref[x1, :, 0:LANES] = real
        mid_ref[x1, :, LANES : 2 * LANES] = imag

    def chunk(c, carry):
        base = pl.multiple_of(c * ROWS, ROWS)
        rows = pl.ds(base, ROWS)
        ky = ky_ref[rows, :]
        for field in range(3):
            at = pl.ds(pl.multiple_of(field * kyl + base, ROWS), ROWS)
            terms = [(mid_ref[x1, at, 0:LANES], mid_ref[x1, at, LANES : 2 * LANES]) for x1 in range(radix)]
            for a, pair in enumerate(butterfly(terms, -1.0)):
                cols = slice(a * LANES, (a + 1) * LANES)
                kx = wave_ref[:, cols]
                keep = mask_ref[rows, cols] != 0
                decay = viscosity * (2.0 + kx * kx + ky * ky)
                fresh = []
                for part in range(2):
                    speed = vel_ref[field, part, rows, cols]
                    change = jnp.where(keep, pair[part], 0.0)
                    change = change + viscosity * side_ref[field, part, rows, cols] - decay * speed
                    fresh.append(speed + time_step * change)
                    next_ref[field, part, rows, cols] = fresh[part]
                if field == 0:
                    div_ref[0, rows, cols] = -kx * fresh[1]
                    div_ref[1, rows, cols] = kx * fresh[0]
                elif field == 1:
                    div_ref[0, rows, cols] = div_ref[0, rows, cols] - ky * fresh[1]
                    div_ref[1, rows, cols] = div_ref[1, rows, cols] + ky * fresh[0]
                else:
                    w_ref[0, rows, cols] = fresh[0]
                    w_ref[1, rows, cols] = fresh[1]
        return carry

    lax.fori_loop(0, kyl // ROWS, chunk, 0)


def neighbours(block, axis):
    count = lax.axis_size(axis)
    if count == 1:
        return jnp.zeros_like(block), jnp.zeros_like(block)
    if count == 2:
        other = lax.ppermute(block, axis, [(0, 1), (1, 0)])
        sign = jnp.where(lax.axis_index(axis) == 0, 1.0, -1.0).astype(jnp.float32)
        return other, sign * other
    forward = [(i, i + 1) for i in range(count - 1)]
    below = lax.ppermute(block, axis, forward)
    above = lax.ppermute(block, axis, [(j, i) for i, j in forward])
    return above + below, above - below


def call(kernel, out, scratch, *args):
    return pl.pallas_call(
        kernel,
        out_shape=out,
        scratch_shapes=scratch,
        compiler_params=pltpu.CompilerParams(vmem_limit_bytes=40 * 2**20),
    )(*args)


def on_device(velocity, mode_mask):
    groups = lax.axis_size("pa")
    rank = lax.axis_index("pa")
    depth, kyl, ncols = velocity.shape[1], velocity.shape[3], velocity.shape[4]
    assert depth == 1
    lines = ncols // groups
    half = kyl * groups
    radix = ncols // LANES
    quarter = half // 2
    pieces = HALF // lines
    table = tables(ncols, half, lines)
    f32 = functools.partial(jax.ShapeDtypeStruct, dtype=jnp.float32)
    bf16 = jnp.bfloat16
    speed = velocity[:, 0]
    side, _ = neighbours(speed, "gz")

    def exchange(block):
        return lax.all_to_all(block, "pa", split_axis=0, concat_axis=0, tiled=True)

    def deal(block):
        if pieces == 1:
            return block
        count, rows, _ = block.shape
        block = block.reshape(count, rows, pieces, 2 * lines)
        return jnp.swapaxes(block, 1, 2).reshape(count * pieces, rows, 2 * lines)

    def gather(block):
        if pieces == 1:
            return block
        rows = block.shape[1]
        block = block.reshape(groups // pieces, pieces, rows, 2 * lines)
        return jnp.swapaxes(block, 1, 2).reshape(groups // pieces, rows, LANES)

    def widen(block):
        if lines == HALF:
            return block
        parts = [jnp.pad(p, ((0, 0), (0, 0), (0, HALF - lines))) for p in (block[..., :lines], block[..., lines:])]
        return jnp.concatenate(parts, -1)

    def narrow(block):
        if lines == HALF:
            return block
        return jnp.concatenate([block[..., :lines], block[..., HALF : HALF + lines]], -1)

    sent = call(
        x_forward_kernel,
        f32((2 * radix, 5 * kyl, LANES)),
        [pltpu.VMEM((radix, 5 * kyl, 2 * LANES), jnp.float32)],
        speed,
        table["wave"],
        table["turns"],
        table["forward"],
    )
    received = exchange(deal(sent))
    _, across = neighbours(received[:, : 2 * kyl], "gz")
    sent = call(
        grid_kernel,
        f32((groups, 3 * kyl, LANES)),
        [
            pltpu.VMEM((half, 12 * LANES), bf16),
            pltpu.VMEM((half, 12 * LANES), bf16),
            pltpu.VMEM((quarter, 6 * LANES), bf16),
            pltpu.VMEM((quarter, 6 * LANES), bf16),
        ],
        widen(received),
        widen(0.5 * across),
        table["to_grid"],
        table["from_grid"],
        table["column"],
    )
    received = gather(exchange(narrow(sent)))
    own_modes = rank * kyl + jnp.arange(kyl, dtype=jnp.int32)
    ky = (2.0 * math.pi / (2 * half)) * own_modes.astype(jnp.float32)
    following, partial, w_next = call(
        x_backward_kernel,
        (f32(speed.shape), f32(speed.shape[1:]), f32(speed.shape[1:])),
        [pltpu.VMEM((radix, 3 * kyl, 2 * LANES), jnp.float32)],
        received,
        speed,
        side,
        mode_mask,
        jnp.broadcast_to(ky[:, None], (kyl, LANES)),
        table["wave"],
        table["turns"],
        table["backward"],
    )
    _, across = neighbours(w_next, "gz")
    divergence = partial + 0.5 * across
    return following[:, None], divergence[None]


def solution(mesh):
    placed = (P(None, "gz", None, "pa", None), P("pa", None))
    return jax.shard_map(
        on_device,
        mesh=mesh,
        in_specs=placed,
        out_specs=(P(None, "gz", None, "pa", None), P("gz", None, "pa", None)),
        check_vma=False,
    )
```

profile of v0, /device:TPU:0, one launch (start us, length us, event | category | flops | bytes accessed | tf_op | source)
XLA Modules:
  0.0 82.3 jit_solution(8272173867620879279)
XLA Ops:
  0.6 0.0 copy-start
  0.6 1.1 %copy-done = f32[3,1,2,32,1024]{4,3,2,1,0:T(8,128)S(1)} copy-done((f32[3,1,2,32,1024]{4,3,2,1,0:T(8,128)S(1)}, f32[3,1,2,32,1024]{4,3,2,1,0:T(8,128)}, u32[]{:S(2)}) %copy-start) | copy-done | bytes 786456
  1.8 0.9 %copy-done.4 = bf16[2,256,256]{2,1,0:T(8,128)(2,1)S(1)} copy-done((bf16[2,256,256]{2,1,0:T(8,128)(2,1)S(1)}, bf16[2,256,256]{2,1,0:T(8,128)(2,1)}, u32[]{:S(2)}) %copy-start.4) | copy-done | bytes 262168
  2.7 0.8 copy-done.6
  3.5 0.7 copy-done.10
  4.2 1.0 %shard_map.104 = f32[16,160,128]{2,1,0:T(8,128)S(1)} custom-call(f32[3,2,32,1024]{3,2,1,0:T(8,128)S(1)} %bitcast.6, f32[8,1024]{1,0:T(8,128)S(1)} %copy-done.6, f32[16,128]{1,0:T(8,128)S(1)} %copy-done.10, bf16[2,256,256]{2,1,0:T(8,128)(2,1)S(1)} %copy-done.4), custom_call_target="tpu_custom_call" | custom-call | tf_op jit(solution)/shard_map/pallas_call | solution.py:333
  5.2 40.7 %all_to_all.10.recv_ref = f32[16,160,128]{2,1,0:T(8,128)S(1)} all-to-all(f32[16,160,128]{2,1,0:T(8,128)S(1)} %shard_map.104), channel_id=1, replica_groups=mesh['gz'=2,'pa'=16] {'pa'}, dimensions={0} | all-to-all | bytes 2621440 | tf_op jit(solution)/shard_map/all_to_all | solution.py:358
  45.9 0.1 collective-permute-start
  46.0 1.9 %collective-permute-done = f32[16,64,128]{2,1,0:T(8,128)S(1)} collective-permute-done((f32[16,64,128]{2,1,0:T(8,128)S(1)}, f32[16,64,128]{2,1,0:T(8,128)S(1)}, u32[]{:S(2)}, u32[]{:S(2)}) %collective-permute-start) | collective-permute-done | bytes 524320 | tf_op jit(solution)/shard_map/ppermute | solution.py:323
  47.9 0.0 copy-done.2
  47.9 0.0 copy-done.3
  47.9 6.2 %shard_map.105 = f32[16,96,128]{2,1,0:T(8,128)} custom-call(f32[16,160,128]{2,1,0:T(8,128)S(1)} %all_to_all.10.recv_ref, f32[16,64,128]{2,1,0:T(8,128)S(1)} %multiply_multiply_fusion.wall_ref, bf16[2,256,512]{2,1,0:T(8,128)(2,1)S(1)} %copy-done.2, bf16[2,512,256]{2,1,0:T(8,128)(2,1)S(1)} %copy-done.3, f32[256,128]{1,0:T(8,128)S(1)} %copy-done.9), custom_call_target="tpu_custom_call" | custom-call | tf_op jit(solution)/shard_map/pallas_call | solution.py:333
  54.1 0.0 copy-start.11
  54.2 3.8 %all-to-all-start.1 = ((f32[16,96,128]{2,1,0:T(8,128)}), f32[16,96,128]{2,1,0:T(8,128)S(1)}, u32[]{:S(2)}, u32[]{:S(2)}) async-start(f32[16,96,128]{2,1,0:T(8,128)} %shard_map.105), calls=%async_computation.1 | async-start | bytes 1572864 | tf_op jit(solution)/shard_map/all_to_all | solution.py:358
  57.9 0.2 collective-permute-start.1
  58.1 2.1 %collective-permute-done.1.side_ref = f32[3,2,32,1024]{3,2,1,0:T(8,128)S(1)} collective-permute-done((f32[3,2,32,1024]{3,2,1,0:T(8,128)S(1)}, f32[3,2,32,1024]{3,2,1,0:T(8,128)S(1)}, u32[]{:S(2)}, u32[]{:S(2)}) %collective-permute-start.1) | collective-permute-done | bytes 786464 | tf_op jit(solution)/shard_map/ppermute | solution.py:323
  60.3 17.7 %all-to-all-done.1.recv_ref = f32[16,96,128]{2,1,0:T(8,128)S(1)} async-done(((f32[16,96,128]{2,1,0:T(8,128)}), f32[16,96,128]{2,1,0:T(8,128)S(1)}, u32[]{:S(2)}, u32[]{:S(2)}) %all-to-all-start.1) | async-done | bytes 786464 | tf_op jit(solution)/shard_map/all_to_all | solution.py:358
  78.0 0.1 broadcast_in_dim.12.ky_ref
  78.0 0.0 copy-done.5
  78.0 0.0 copy-done.8
  78.1 1.9 %shard_map.106 = (f32[3,2,32,1024]{3,2,1,0:T(8,128)}, f32[2,32,1024]{2,1,0:T(8,128)S(1)}, f32[2,32,1024]{2,1,0:T(8,128)S(1)}) custom-call(f32[16,96,128]{2,1,0:T(8,128)S(1)} %all-to-all-done.1.recv_ref, f32[3,2,32,1024]{3,2,1,0:T(8,128)S(1)} %bitcast.8, f32[3,2,32,1024]{3,2,1,0:T(8,128)S(1)} %collective-permute-done.1.side_ref, s32[32,1024]{1,0:T(8,128)S(1)} %copy-done.8, ...), custom_call_target="tpu_custom_call" | custom-call | tf_op jit(solution)/shard_map/pallas_call | solution.py:333
  80.0 0.0 collective-permute-start.2
  80.0 1.5 %collective-permute-done.2 = f32[2,32,1024]{2,1,0:T(8,128)S(1)} collective-permute-done((f32[2,32,1024]{2,1,0:T(8,128)S(1)}, f32[2,32,1024]{2,1,0:T(8,128)S(1)}, u32[]{:S(2)}, u32[]{:S(2)}) %collective-permute-start.2) | collective-permute-done | bytes 262176 | tf_op jit(solution)/shard_map/ppermute | solution.py:323
  81.5 0.7 add_bitcast_fusion
  (17 shorter events, 0.1 us)
Async XLA Ops:
  0.6 1.1 %copy-start = (f32[3,1,2,32,1024]{4,3,2,1,0:T(8,128)S(1)}, f32[3,1,2,32,1024]{4,3,2,1,0:T(8,128)}, u32[]{:S(2)}) copy-start(f32[3,1,2,32,1024]{4,3,2,1,0:T(8,128)} %param.9) | copy-start | bytes 2359300
  1.8 0.9 %copy-start.4 = (bf16[2,256,256]{2,1,0:T(8,128)(2,1)S(1)}, bf16[2,256,256]{2,1,0:T(8,128)(2,1)}, u32[]{:S(2)}) copy-start(bf16[2,256,256]{2,1,0:T(8,128)(2,1)} %constant.38.clone.mat_ref) | copy-start | bytes 786436
  2.7 0.8 copy-start.6
  3.5 0.7 copy-start.10
  45.8 2.1 %copy-start.2 = (bf16[2,256,512]{2,1,0:T(8,128)(2,1)S(1)}, bf16[2,256,512]{2,1,0:T(8,128)(2,1)}, u32[]{:S(2)}) copy-start(bf16[2,256,512]{2,1,0:T(8,128)(2,1)} %constant.39.clone.to_ref) | copy-start | bytes 1572868
  45.8 2.1 %copy-start.3 = (bf16[2,512,256]{2,1,0:T(8,128)(2,1)S(1)}, bf16[2,512,256]{2,1,0:T(8,128)(2,1)}, u32[]{:S(2)}) copy-start(bf16[2,512,256]{2,1,0:T(8,128)(2,1)} %constant.40.clone.from_ref) | copy-start | bytes 1572868
  45.8 2.1 %copy-start.9 = (f32[256,128]{1,0:T(8,128)S(1)}, f32[256,128]{1,0:T(8,128)}, u32[]{:S(2)}) copy-start(f32[256,128]{1,0:T(8,128)} %constant.41.clone.column_ref) | copy-start | bytes 393220
  45.9 2.0 %collective-permute-start = (f32[16,64,128]{2,1,0:T(8,128)S(1)}, f32[16,64,128]{2,1,0:T(8,128)S(1)}, u32[]{:S(2)}, u32[]{:S(2)}) collective-permute-start(f32[16,64,128]{2,1,0:T(8,128)S(1)} %slice.4), channel_id=1, source_target_pairs={{0,16},{16,0},{1,17},{17,1},{2,18},{18,2},{3,19},{19,3},{4,20},{20... | collective-permute-start | bytes 1572872 | tf_op jit(solution)/shard_map/ppermute | solution.py:323
  54.1 3.8 %copy-start.1 = (f32[3,1,2,32,1024]{4,3,2,1,0:T(8,128)S(1)}, f32[3,1,2,32,1024]{4,3,2,1,0:T(8,128)}, u32[]{:S(2)}) copy-start(f32[3,1,2,32,1024]{4,3,2,1,0:T(8,128)} %param.9) | copy-start | bytes 2359300
  54.1 23.9 %copy-start.5 = (bf16[2,256,256]{2,1,0:T(8,128)(2,1)S(1)}, bf16[2,256,256]{2,1,0:T(8,128)(2,1)}, u32[]{:S(2)}) copy-start(bf16[2,256,256]{2,1,0:T(8,128)(2,1)} %constant.42.clone.mat_ref) | copy-start | bytes 786436
  54.1 23.9 %copy-start.7 = (f32[8,1024]{1,0:T(8,128)S(1)}, f32[8,1024]{1,0:T(8,128)}, u32[]{:S(2)}) copy-start(f32[8,1024]{1,0:T(8,128)} %constant.36.clone.wave_ref) | copy-start | bytes 98308
  54.1 23.9 %copy-start.8 = (s32[32,1024]{1,0:T(8,128)S(1)}, s32[32,1024]{1,0:T(8,128)}, u32[]{:S(2)}) copy-start(s32[32,1024]{1,0:T(8,128)} %mask_ref.1) | copy-start | bytes 393220
  54.1 23.9 %copy-start.11 = (f32[16,128]{1,0:T(8,128)S(1)}, f32[16,128]{1,0:T(8,128)}, u32[]{:S(2)}) copy-start(f32[16,128]{1,0:T(8,128)} %constant.37.clone.turn_ref) | copy-start | bytes 24580
  54.2 23.8 %all-to-all-start.1 = ((f32[16,96,128]{2,1,0:T(8,128)}), f32[16,96,128]{2,1,0:T(8,128)S(1)}, u32[]{:S(2)}, u32[]{:S(2)}) async-start(f32[16,96,128]{2,1,0:T(8,128)} %shard_map.105), calls=%async_computation.1 | async-start | bytes 1572864 | tf_op jit(solution)/shard_map/all_to_all | solution.py:358
  57.9 2.4 %collective-permute-start.1 = (f32[3,2,32,1024]{3,2,1,0:T(8,128)S(1)}, f32[3,2,32,1024]{3,2,1,0:T(8,128)S(1)}, u32[]{:S(2)}, u32[]{:S(2)}) collective-permute-start(f32[3,2,32,1024]{3,2,1,0:T(8,128)S(1)} %bitcast.7), channel_id=1, source_target_pairs={{0,16},{16,0},{1,17},{17,1},{2,18},{18,2},{3,19},{19,3},{4,20},{20... | collective-permute-start | bytes 2359304 | tf_op jit(solution)/shard_map/ppermute | solution.py:323
  80.0 1.5 %collective-permute-start.2 = (f32[2,32,1024]{2,1,0:T(8,128)S(1)}, f32[2,32,1024]{2,1,0:T(8,128)S(1)}, u32[]{:S(2)}, u32[]{:S(2)}) collective-permute-start(f32[2,32,1024]{2,1,0:T(8,128)S(1)} %get-tuple-element.7), channel_id=1, source_target_pairs={{0,16},{16,0},{1,17},{17,1},{2,18},{18,2},{3,19},{19,3},{4,20},{20... | collective-permute-start | bytes 786440 | tf_op jit(solution)/shard_map/ppermute | solution.py:323
where the time goes:
time: 82.7 us; the launch traced here: 82.3 us
  blocking collectives  40.7 us (49%)
  waiting for transfers between devices  23.2 us (28%)
  Pallas kernels  9.11 us (11%)
  starting transfers between devices  4.03 us (5%)
  local copies, waits for them, and re-layouts  3.67 us (4%)
    all_to_all x1, blocking collectives, exchange(): return lax.all_to_all(block, 'pa', split_axis=0, concat_axis=0, tiled=True)  40.7 us
    all_to_all x1, waiting for transfers between devices, exchange(): return lax.all_to_all(block, 'pa', split_axis=0, concat_axis=0, tiled=True)  17.7 us
    pallas_call x3, Pallas kernels, call(): pl.pallas_call(kernel, out_shape=out, scratch_shapes=scratch, compiler_pa...  9.11 us
    ppermute x3, waiting for transfers between devices, neighbours(): other = lax.ppermute(block, axis, [(0, 1), (1, 0)])  5.56 us
    all_to_all x1, starting transfers between devices, exchange(): return lax.all_to_all(block, 'pa', split_axis=0, concat_axis=0, tiled=True)  3.76 us
    unnamed x24, local copies, waits for them, and re-layouts  3.56 us
  transfers between devices with their start and end apart: 4, of which 4 were waited for; matrix products, arithmetic and copies ran while one was open for 0% of the time, Pallas kernels for 0%

commit v1 on v0

v1 whole, which is shorter than its diff:
```python
import functools
import math

import jax
import jax.numpy as jnp
import ml_dtypes
import numpy as np
from jax import lax
from jax.experimental import pallas as pl
from jax.experimental.pallas import tpu as pltpu
from jax.sharding import PartitionSpec as P

time_step = 0.2
viscosity = 0.25
LANES = 128
HALF = LANES // 2
ROWS = 8


def halves(table):
    high = table.astype(np.float32).astype(ml_dtypes.bfloat16)
    low = (table - high.astype(np.float64)).astype(np.float32).astype(ml_dtypes.bfloat16)
    return np.stack([high, low])


def wheel(rows, cols, period):
    angle = 2.0 * np.pi / period * (np.outer(rows, cols) % period)
    return np.cos(angle), np.sin(angle)


@functools.lru_cache(maxsize=None)
def tables(ncols, half, lines):
    radix = ncols // LANES
    lane = np.arange(LANES)
    scale = 1.0 / math.sqrt(ncols)
    cos, sin = wheel(lane, lane, LANES)
    forward = np.zeros((2 * LANES, 2 * LANES))
    for part in range(LANES // lines):
        x2 = np.arange(part * lines, (part + 1) * lines)
        at = part * 2 * lines
        forward[:LANES, at : at + lines] = cos[:, x2]
        forward[LANES:, at : at + lines] = -sin[:, x2]
        forward[:LANES, at + lines : at + 2 * lines] = sin[:, x2]
        forward[LANES:, at + lines : at + 2 * lines] = cos[:, x2]
    backward = forward.T
    turn_cos, turn_sin = wheel(np.arange(radix), lane, ncols)
    turns = np.concatenate([turn_cos, turn_sin]).astype(np.float32)
    quarter = half // 2
    nrows = 2 * half
    b = np.arange(quarter)
    yscale = 1.0 / math.sqrt(nrows)
    ycos, ysin = wheel(b, b, quarter)
    to_grid = 2.0 * yscale * np.concatenate([ycos, -ysin], 1)
    from_grid = yscale * np.concatenate([ycos, -ysin], 0)
    column = np.zeros((quarter, LANES))
    for y1 in range(1, 4):
        c, s = wheel(b, np.array([y1]), nrows)
        column[:, 2 * y1] = c[:, 0]
        column[:, 2 * y1 + 1] = s[:, 0]
    modes = np.arange(ncols)
    signed = np.where(modes < ncols // 2, modes, modes - ncols).astype(np.float32)
    wave = np.broadcast_to(np.float32(2.0 * math.pi / ncols) * signed, (ROWS, ncols))
    return dict(
        forward=halves(forward * scale),
        backward=halves(backward * scale),
        turns=turns,
        to_grid=halves(to_grid),
        from_grid=halves(from_grid),
        column=column.astype(np.float32),
        wave=np.ascontiguousarray(wave),
    )


def split(value):
    high = value.astype(jnp.bfloat16)
    low = (value - high.astype(jnp.float32)).astype(jnp.bfloat16)
    return high, low


def product(a_high, a_low, b_high, b_low):
    dot = functools.partial(jnp.dot, preferred_element_type=jnp.float32)
    return dot(a_high, b_low) + dot(a_low, b_high) + dot(a_high, b_high)


def butterfly(terms, sign):
    count = len(terms)
    if count == 1:
        return terms
    even = butterfly(terms[0::2], sign)
    odd = butterfly(terms[1::2], sign)
    first, second = [], []
    for k in range(count // 2):
        real, imag = odd[k]
        if k == 0:
            pass
        elif 4 * k == count:
            real, imag = -sign * imag, sign * real
        elif 8 * k == count:
            root = math.sqrt(0.5)
            real, imag = root * (real - sign * imag), root * (imag + sign * real)
        elif 8 * k == 3 * count:
            root = math.sqrt(0.5)
            real, imag = -root * (real + sign * imag), root * (sign * real - imag)
        else:
            c = math.cos(2.0 * math.pi * k / count)
            s = sign * math.sin(2.0 * math.pi * k / count)
            real, imag = c * real - s * imag, s * real + c * imag
        first.append((even[k][0] + real, even[k][1] + imag))
        second.append((even[k][0] - real, even[k][1] - imag))
    return first + second


def x_forward_kernel(plan, vel_ref, wave_ref, turn_ref, mat_ref, out_ref, mid_ref):
    kyl, ncols = vel_ref.shape[2:]
    radix = ncols // LANES
    cols = [slice(a * LANES, (a + 1) * LANES) for a in range(radix)]

    def chunk(c, carry):
        base = pl.multiple_of(c * ROWS, ROWS)
        rows = pl.ds(base, ROWS)
        for slot, (field, slope) in enumerate(plan):
            terms = [(vel_ref[field, 0, rows, s], vel_ref[field, 1, rows, s]) for s in cols]
            if slope:
                terms = [(-wave_ref[:, s] * imag, wave_ref[:, s] * real) for s, (real, imag) in zip(cols, terms)]
            at = pl.ds(pl.multiple_of(slot * kyl + base, ROWS), ROWS)
            for x1, (real, imag) in enumerate(butterfly(terms, 1.0)):
                if x1:
                    cos = turn_ref[x1 : x1 + 1, :]
                    sin = turn_ref[radix + x1 : radix + x1 + 1, :]
                    real, imag = real * cos - imag * sin, real * sin + imag * cos
                mid_ref[x1, at, 0:LANES] = real
                mid_ref[x1, at, LANES : 2 * LANES] = imag
        return carry

    lax.fori_loop(0, kyl // ROWS, chunk, 0)
    for x1 in range(radix):
        high, low = split(mid_ref[x1])
        lines = product(high, low, mat_ref[0], mat_ref[1])
        out_ref[2 * x1] = lines[:, :LANES]
        out_ref[2 * x1 + 1] = lines[:, LANES:]


BLOCK = 32


def swap(value):
    return pltpu.roll(value, HALF, 1)


def left_half(rows):
    return lax.broadcasted_iota(jnp.int32, (rows, LANES), 1) < HALF


def fill(quarter, pairs_at, column_ref, high_ref, low_ref):
    def block(c, carry):
        base = pl.multiple_of(c * BLOCK, BLOCK)
        rows = pl.ds(base, BLOCK)
        lower = pl.ds(pl.multiple_of(quarter + base, BLOCK), BLOCK)
        column = lambda k: jnp.broadcast_to(column_ref[rows, k : k + 1], (BLOCK, LANES))
        near, far = pairs_at(c, 0), pairs_at(c, 1)
        count = len(near)
        for pair in range(count):
            a_re, a_im = near[pair]
            b_re, b_im = far[pair]
            sums = (
                (a_re + b_re, a_im + b_im),
                (a_re - b_im, a_im + b_re),
                (a_re - b_re, a_im - b_im),
                (a_re + b_im, a_im - b_re),
            )
            for y1, (real, imag) in enumerate(sums):
                if y1:
                    cos = column(2 * y1)
                    sin = column(2 * y1 + 1)
                    real, imag = real * cos - imag * sin, real * sin + imag * cos
                at = slice((count * y1 + pair) * LANES, (count * y1 + pair + 1) * LANES)
                high_ref[rows, at], low_ref[rows, at] = split(real)
                high_ref[lower, at], low_ref[lower, at] = split(imag)
        return carry

    lax.fori_loop(0, quarter // BLOCK, block, 0)


def reader(groups, kyl, quarter):
    each = BLOCK // kyl
    left = left_half(BLOCK)

    def load(ref, f, c, far):
        sources = pl.ds(c * each + far * (groups // 2), each)
        return ref[sources, f * kyl : (f + 1) * kyl, :].reshape(BLOCK, LANES)

    def modes(c, far):
        index = c * BLOCK + far * quarter + lax.broadcasted_iota(jnp.int32, (BLOCK, LANES), 0)
        ky = index.astype(jnp.float32) * (2.0 * math.pi / (4 * quarter))
        return jnp.where(index == 0, 0.5, 1.0), jnp.where(left, -ky, ky)

    def paired(one, two, weight):
        one = one * weight
        two = two * weight
        return jnp.where(left, one, swap(two)), jnp.where(left, swap(one), two)

    return load, modes, paired


def speed_kernel(uv_ref, to_ref, column_ref, grid_ref, high_ref, low_ref):
    groups, kyl = uv_ref.shape[0], uv_ref.shape[1] // 2
    quarter = groups * kyl // 2
    load, modes, paired = reader(groups, kyl, quarter)

    def pairs_at(c, far):
        weight, _ = modes(c, far)
        return [paired(load(uv_ref, 0, c, far), load(uv_ref, 1, c, far), weight)]

    fill(quarter, pairs_at, column_ref, high_ref, low_ref)
    grid_ref[...] = product(to_ref[0], to_ref[1], high_ref[...], low_ref[...])


def cross_kernel(uv_ref, wall_ref, rest_ref, grid_ref, to_ref, from_ref, column_ref, out_ref, yx_high, yx_low, high_ref, low_ref, z_high, z_low):
    groups, kyl = uv_ref.shape[0], uv_ref.shape[1] // 2
    quarter = groups * kyl // 2
    load, modes, paired = reader(groups, kyl, quarter)

    def pairs_at(c, far):
        weight, ky = modes(c, far)
        u = load(uv_ref, 0, c, far)
        du_dz, dv_dz = load(wall_ref, 0, c, far), load(wall_ref, 1, c, far)
        w, dw, dv = [load(rest_ref, f, c, far) for f in range(3)]
        omega_x = ky * swap(w) - dv_dz
        omega_y = du_dz - dw
        omega_z = dv - ky * swap(u)
        return [paired(omega_x, omega_y, weight), paired(w, omega_z, weight)]

    fill(quarter, pairs_at, column_ref, high_ref, low_ref)
    wide = left_half(quarter)
    kept = None
    for y1 in range(4):
        at = slice(2 * y1 * LANES, 2 * (y1 + 1) * LANES)
        grid = product(to_ref[0], to_ref[1], high_ref[:, at], low_ref[:, at])
        slot = slice(y1 * LANES, (y1 + 1) * LANES)
        uv = grid_ref[:, slot]
        xy = grid[:, :LANES]
        wz = grid[:, LANES:]
        zw = swap(wz)
        h_yx = jnp.where(wide, wz, zw) * xy - jnp.where(wide, zw, wz) * uv
        spin = uv * swap(xy)
        h_z = spin - swap(spin)
        yx_high[:, slot], yx_low[:, slot] = split(h_yx)
        if y1 % 2 == 0:
            kept = h_z
        else:
            slot = slice(y1 // 2 * LANES, (y1 // 2 + 1) * LANES)
            z_high[:, slot], z_low[:, slot] = split(jnp.where(wide, kept, -h_z))
    freq = product(from_ref[0], from_ref[1], z_high[...], z_low[...])
    turn = turns_of(column_ref, quarter)
    one = jnp.ones((quarter, LANES), jnp.float32)
    zero = jnp.zeros((quarter, LANES), jnp.float32)
    z01 = piece(freq, quarter, 0, jnp.where(wide, one, turn[1][0]), jnp.where(wide, zero, turn[1][1]))
    z23 = piece(freq, quarter, 1, jnp.where(wide, turn[2][0], turn[3][0]), jnp.where(wide, turn[2][1], turn[3][1]))
    v_re, v_im = z01[0] + z23[0], z01[1] + z23[1]
    d_re, d_im = z01[0] - z23[0], z01[1] - z23[1]
    store(out_ref, kyl, 0, 0, jnp.where(wide, v_re + swap(v_re), v_im + swap(v_im)))
    store(out_ref, kyl, 1, 0, jnp.where(wide, d_re + swap(d_im), swap(d_im) - d_re))


def turns_of(column_ref, quarter):
    column = lambda k: jnp.broadcast_to(column_ref[:, k : k + 1], (quarter, LANES))
    return [(None, None)] + [(column(2 * y1), column(2 * y1 + 1)) for y1 in range(1, 4)]


def piece(freq, quarter, slot, cos, sin):
    real = freq[:quarter, slot * LANES : (slot + 1) * LANES]
    imag = freq[quarter:, slot * LANES : (slot + 1) * LANES]
    if cos is None:
        return real, imag
    return real * cos + imag * sin, imag * cos - real * sin


def store(out_ref, kyl, far, field, value):
    gap = out_ref.shape[0] // 2
    for s in range(gap):
        out_ref[far * gap + s, field * kyl : (field + 1) * kyl, :] = value[s * kyl : (s + 1) * kyl]


def return_kernel(yx_high, yx_low, from_ref, column_ref, out_ref):
    quarter = column_ref.shape[0]
    kyl = out_ref.shape[1] // 2
    wide = left_half(quarter)
    freq = product(from_ref[0], from_ref[1], yx_high[...], yx_low[...])
    turn = turns_of(column_ref, quarter)
    q0, q1, q2, q3 = [piece(freq, quarter, y1, *turn[y1]) for y1 in range(4)]
    near_re = q0[0] + q1[0] + q2[0] + q3[0]
    near_im = q0[1] + q1[1] + q2[1] + q3[1]
    far_re = q0[0] + q1[1] - q2[0] - q3[1]
    far_im = q0[1] - q1[0] - q2[1] + q3[0]
    for far, real, imag in ((0, near_re, near_im), (1, far_re, far_im)):
        store(out_ref, kyl, far, 0, -jnp.where(wide, swap(real), imag))
        store(out_ref, kyl, far, 1, jnp.where(wide, real, swap(imag)))


def to_modes(recv_ref, turn_ref, mat_ref, mid_ref):
    radix = mid_ref.shape[0]
    for x1 in range(radix):
        high, low = split(jnp.concatenate([recv_ref[2 * x1], recv_ref[2 * x1 + 1]], axis=1))
        freq = product(high, low, mat_ref[0], mat_ref[1])
        real = freq[:, :LANES]
        imag = freq[:, LANES:]
        if x1:
            cos = turn_ref[x1 : x1 + 1, :]
            sin = turn_ref[radix + x1 : radix + x1 + 1, :]
            real, imag = real * cos + imag * sin, imag * cos - real * sin
        mid_ref[x1, :, 0:LANES] = real
        mid_ref[x1, :, LANES : 2 * LANES] = imag


def advance(field, slot, kyl, base, vel_ref, side_ref, mask_ref, ky_ref, wave_ref, mid_ref):
    radix = mid_ref.shape[0]
    rows = pl.ds(base, ROWS)
    ky = ky_ref[rows, :]
    at = pl.ds(pl.multiple_of(slot * kyl + base, ROWS), ROWS)
    terms = [(mid_ref[x1, at, 0:LANES], mid_ref[x1, at, LANES : 2 * LANES]) for x1 in range(radix)]
    for a, pair in enumerate(butterfly(terms, -1.0)):
        cols = slice(a * LANES, (a + 1) * LANES)
        kx = wave_ref[:, cols]
        keep = mask_ref[rows, cols] != 0
        decay = viscosity * (2.0 + kx * kx + ky * ky)
        fresh = []
        for part in range(2):
            speed = vel_ref[field, part, rows, cols]
            change = jnp.where(keep, pair[part], 0.0)
            change = change + viscosity * side_ref[field, part, rows, cols] - decay * speed
            fresh.append(speed + time_step * change)
        yield cols, kx, ky, fresh[0], fresh[1]


def wall_kernel(recv_ref, vel_ref, side_ref, mask_ref, ky_ref, wave_ref, turn_ref, mat_ref, w_ref, mid_ref):
    kyl = vel_ref.shape[2]
    to_modes(recv_ref, turn_ref, mat_ref, mid_ref)

    def chunk(c, carry):
        base = pl.multiple_of(c * ROWS, ROWS)
        rows = pl.ds(base, ROWS)
        for cols, _, _, real, imag in advance(2, 0, kyl, base, vel_ref, side_ref, mask_ref, ky_ref, wave_ref, mid_ref):
            w_ref[0, rows, cols] = real
            w_ref[1, rows, cols] = imag
        return carry

    lax.fori_loop(0, kyl // ROWS, chunk, 0)


def final_kernel(recv_ref, vel_ref, side_ref, mask_ref, ky_ref, wave_ref, turn_ref, mat_ref, w_ref, across_ref, sign_ref, next_ref, div_ref, mid_ref):
    kyl = vel_ref.shape[2]
    to_modes(recv_ref, turn_ref, mat_ref, mid_ref)
    next_ref[2] = w_ref[...]
    sign = sign_ref[0:1, :]

    def chunk(c, carry):
        base = pl.multiple_of(c * ROWS, ROWS)
        rows = pl.ds(base, ROWS)
        shared = (kyl, base, vel_ref, side_ref, mask_ref, ky_ref, wave_ref, mid_ref)
        for one, two in zip(advance(0, 0, *shared), advance(1, 1, *shared)):
            cols, kx, ky, u_re, u_im = one
            v_re, v_im = two[3:]
            next_ref[0, 0, rows, cols] = u_re
            next_ref[0, 1, rows, cols] = u_im
            next_ref[1, 0, rows, cols] = v_re
            next_ref[1, 1, rows, cols] = v_im
            div_ref[0, rows, cols] = sign * across_ref[0, rows, cols] - kx * u_im - ky * v_im
            div_ref[1, rows, cols] = sign * across_ref[1, rows, cols] + kx * u_re + ky * v_re
        return carry

    lax.fori_loop(0, kyl // ROWS, chunk, 0)


def neighbours(block, axis):
    count = lax.axis_size(axis)
    if count == 1:
        return jnp.zeros_like(block), jnp.zeros_like(block), jnp.float32(1.0)
    if count == 2:
        other = lax.ppermute(block, axis, [(0, 1), (1, 0)])
        return other, other, jnp.where(lax.axis_index(axis) == 0, 1.0, -1.0).astype(jnp.float32)
    forward = [(i, i + 1) for i in range(count - 1)]
    below = lax.ppermute(block, axis, forward)
    above = lax.ppermute(block, axis, [(j, i) for i, j in forward])
    return above + below, above - below, jnp.float32(1.0)


def call(kernel, out, scratch, *args):
    return pl.pallas_call(
        kernel,
        out_shape=out,
        scratch_shapes=scratch,
        compiler_params=pltpu.CompilerParams(vmem_limit_bytes=40 * 2**20),
    )(*args)


def on_device(velocity, mode_mask):
    groups = lax.axis_size("pa")
    rank = lax.axis_index("pa")
    depth, kyl, ncols = velocity.shape[1], velocity.shape[3], velocity.shape[4]
    assert depth == 1
    lines = ncols // groups
    half = kyl * groups
    radix = ncols // LANES
    quarter = half // 2
    pieces = HALF // lines
    table = tables(ncols, half, lines)
    f32 = functools.partial(jax.ShapeDtypeStruct, dtype=jnp.float32)
    bf16 = jnp.bfloat16
    speed = velocity[:, 0]
    side, _, _ = neighbours(speed, "gz")

    def exchange(block):
        return lax.all_to_all(block, "pa", split_axis=0, concat_axis=0, tiled=True)

    def deal(block):
        if pieces == 1:
            return block
        count, rows, _ = block.shape
        block = block.reshape(count, rows, pieces, 2 * lines)
        return jnp.swapaxes(block, 1, 2).reshape(count * pieces, rows, 2 * lines)

    def gather(block):
        if pieces == 1:
            return block
        rows = block.shape[1]
        block = block.reshape(groups // pieces, pieces, rows, 2 * lines)
        return jnp.swapaxes(block, 1, 2).reshape(groups // pieces, rows, LANES)

    def widen(block):
        if lines == HALF:
            return block
        parts = [jnp.pad(p, ((0, 0), (0, 0), (0, HALF - lines))) for p in (block[..., :lines], block[..., lines:])]
        return jnp.concatenate(parts, -1)

    def narrow(block):
        if lines == HALF:
            return block
        return jnp.concatenate([block[..., :lines], block[..., HALF : HALF + lines]], -1)

    x_tables = (table["wave"], table["turns"], table["forward"])

    def x_forward(*plan):
        count = len(plan) * kyl
        scratch = [pltpu.VMEM((radix, count, 2 * LANES), jnp.float32)]
        kernel = functools.partial(x_forward_kernel, plan)
        return exchange(deal(call(kernel, f32((2 * radix, count, LANES)), scratch, speed, *x_tables)))

    uv = x_forward((0, False), (1, False))
    rest = x_forward((2, False), (2, True), (1, True))
    _, across, sign = neighbours(uv, "gz")
    uv = widen(uv)
    pair = lambda count: [pltpu.VMEM((half, 4 * count * LANES), bf16)] * 2
    grid_uv = call(
        speed_kernel, f32((quarter, 4 * LANES)), pair(1), uv, table["to_grid"], table["column"]
    )
    packed = jax.ShapeDtypeStruct((quarter, 4 * LANES), bf16)
    sent_z, yx_high, yx_low = call(
        cross_kernel,
        (f32((groups, kyl, LANES)), packed, packed),
        pair(2) + [pltpu.VMEM((quarter, 2 * LANES), bf16)] * 2,
        uv,
        widen(across * (0.5 * sign)),
        widen(rest),
        grid_uv,
        table["to_grid"],
        table["from_grid"],
        table["column"],
    )
    z_lines = gather(exchange(narrow(sent_z)))
    sent_xy = call(
        return_kernel, f32((groups, 2 * kyl, LANES)), [], yx_high, yx_low, table["from_grid"], table["column"]
    )
    xy_lines = gather(exchange(narrow(sent_xy)))
    own_modes = rank * kyl + jnp.arange(kyl, dtype=jnp.int32)
    ky = (2.0 * math.pi / (2 * half)) * own_modes.astype(jnp.float32)
    ky = jnp.broadcast_to(ky[:, None], (kyl, LANES))
    shared = (speed, side, mode_mask, ky, table["wave"], table["turns"], table["backward"])
    mid = lambda count: [pltpu.VMEM((radix, count * kyl, 2 * LANES), jnp.float32)]
    w_next = call(wall_kernel, f32(speed.shape[1:]), mid(1), z_lines, *shared)
    _, across, sign = neighbours(w_next, "gz")
    following, divergence = call(
        final_kernel,
        (f32(speed.shape), f32(speed.shape[1:])),
        mid(2),
        xy_lines,
        *shared,
        w_next,
        across,
        jnp.broadcast_to(0.5 * sign, (ROWS, LANES)),
    )
    return following[:, None], divergence[None]


def solution(mesh):
    placed = (P(None, "gz", None, "pa", None), P("pa", None))
    return jax.shard_map(
        on_device,
        mesh=mesh,
        in_specs=placed,
        out_specs=(P(None, "gz", None, "pa", None), P("gz", None, "pa", None)),
        check_vma=False,
    )
```

time: 82.7 us -> 94.6 us (1.14)
  blocking collectives: 40.7 us -> 0 us
  waiting for transfers between devices: 23.2 us -> 47 us
  starting transfers between devices: 4.03 us -> 21.6 us
  local copies, waits for them, and re-layouts: 3.67 us -> 9.56 us
  Pallas kernels: 9.11 us -> 12.9 us
  other arithmetic: 0.79 us -> 1.97 us
    all_to_all x1 -> x0, blocking collectives: 40.7 us -> none  [exchange(): return lax.all_to_all(block, 'pa', split_axis=0, concat_axis=0, tiled=True)]
    all_to_all x1 -> x4, waiting for transfers between devices: 17.7 us -> 45.5 us  [exchange(): return lax.all_to_all(block, 'pa', split_axis=0, concat_axis=0, tiled=True)]
    all_to_all x1 -> x4, starting transfers between devices: 3.76 us -> 21.3 us  [exchange(): return lax.all_to_all(block, 'pa', split_axis=0, concat_axis=0, tiled=True)]
    unnamed x24 -> x40, local copies, waits for them, and re-layouts: 3.56 us -> 9.49 us
    ppermute x3, waiting for transfers between devices: 5.56 us -> 1.53 us  [neighbours(): other = lax.ppermute(block, axis, [(0, 1), (1, 0)])]
    pallas_call x3 -> x7, Pallas kernels: 9.11 us -> 12.9 us  [call(): pl.pallas_call(kernel, out_shape=out, scratch_shapes=scratch, compiler_pa...]
    mul x1, other arithmetic: 0.04 us -> 1.96 us  [on_device(): across * (0.5 * sign)]
  transfers between devices with their start and end apart: 4 -> 7, of which waited for: 4 -> 5; matrix products, arithmetic and copies ran while one was open for 0% -> 2% of each run, Pallas kernels for 0% -> 6%
where the time goes in v1:
time: 94.6 us; the launch traced here: 93.8 us
  waiting for transfers between devices  47 us (50%)
  starting transfers between devices  21.6 us (23%)
  Pallas kernels  12.9 us (14%)
  local copies, waits for them, and re-layouts  9.56 us (10%)
  other arithmetic  1.97 us (2%)
    all_to_all x4, waiting for transfers between devices, exchange(): return lax.all_to_all(block, 'pa', split_axis=0, concat_axis=0, tiled=True)  45.5 us
    all_to_all x4, starting transfers between devices, exchange(): return lax.all_to_all(block, 'pa', split_axis=0, concat_axis=0, tiled=True)  21.3 us
    pallas_call x7, Pallas kernels, call(): pl.pallas_call(kernel, out_shape=out, scratch_shapes=scratch, compiler_pa...  12.9 us
    unnamed x40, local copies, waits for them, and re-layouts  9.49 us
    mul x1, other arithmetic, on_device(): across * (0.5 * sign)  1.96 us
  transfers between devices with their start and end apart: 7, of which 5 were waited for; matrix products, arithmetic and copies ran while one was open for 2% of the time, Pallas kernels for 6%

profile of v1, /device:TPU:0, one launch (start us, length us, event | category | flops | bytes accessed | tf_op | source)
XLA Modules:
  0.0 93.8 jit_solution(13541322496063964772)
XLA Ops:
  1.3 1.1 %copy-done = f32[3,1,2,32,1024]{4,3,2,1,0:T(8,128)S(1)} copy-done((f32[3,1,2,32,1024]{4,3,2,1,0:T(8,128)S(1)}, f32[3,1,2,32,1024]{4,3,2,1,0:T(8,128)}, u32[]{:S(2)}) %copy-start) | copy-done | bytes 786456
  2.5 0.9 %copy-done.9 = bf16[2,256,256]{2,1,0:T(8,128)(2,1)S(1)} copy-done((bf16[2,256,256]{2,1,0:T(8,128)(2,1)S(1)}, bf16[2,256,256]{2,1,0:T(8,128)(2,1)}, u32[]{:S(2)}) %copy-start.9) | copy-done | bytes 262168
  3.4 0.8 copy-done.11
  4.2 1.6 %shard_map.104 = f32[16,64,128]{2,1,0:T(8,128)} custom-call(f32[3,2,32,1024]{3,2,1,0:T(8,128)S(1)} %bitcast.5, f32[8,1024]{1,0:T(8,128)S(1)} %copy-done.11, f32[16,128]{1,0:T(8,128)S(1)} %copy-done.19, bf16[2,256,256]{2,1,0:T(8,128)(2,1)S(1)} %copy-done.9), custom_call_target="tpu_custom_call" | custom-call | tf_op jit(solution)/shard_map/pallas_call | solution.py:388
  5.8 8.5 %all-to-all-start = ((f32[16,64,128]{2,1,0:T(8,128)}), f32[16,64,128]{2,1,0:T(8,128)S(1)}, u32[]{:S(2)}, u32[]{:S(2)}) async-start(f32[16,64,128]{2,1,0:T(8,128)} %shard_map.104), calls=%async_computation | async-start | bytes 1048576 | tf_op jit(solution)/shard_map/all_to_all | solution.py:413
  14.3 1.7 %shard_map.105 = f32[16,96,128]{2,1,0:T(8,128)} custom-call(f32[3,2,32,1024]{3,2,1,0:T(8,128)S(1)} %bitcast.6, f32[8,1024]{1,0:T(8,128)S(1)} %copy-done.12, f32[16,128]{1,0:T(8,128)S(1)} %copy-done.19, bf16[2,256,256]{2,1,0:T(8,128)(2,1)S(1)} %copy-done.10), custom_call_target="tpu_custom_call" | custom-call | tf_op jit(solution)/shard_map/pallas_call | solution.py:388
  16.0 13.3 %all-to-all-done.uv_ref = f32[16,64,128]{2,1,0:T(8,128)S(1)} async-done(((f32[16,64,128]{2,1,0:T(8,128)}), f32[16,64,128]{2,1,0:T(8,128)S(1)}, u32[]{:S(2)}, u32[]{:S(2)}) %all-to-all-start) | async-done | bytes 524320 | tf_op jit(solution)/shard_map/all_to_all | solution.py:413
  29.3 3.9 %all-to-all-start.1 = ((f32[16,96,128]{2,1,0:T(8,128)}), f32[16,96,128]{2,1,0:T(8,128)S(1)}, u32[]{:S(2)}, u32[]{:S(2)}) async-start(f32[16,96,128]{2,1,0:T(8,128)} %shard_map.105), calls=%async_computation.1 | async-start | bytes 1572864 | tf_op jit(solution)/shard_map/all_to_all | solution.py:413
  33.4 1.6 %shard_map.106.grid_ref = f32[256,512]{1,0:T(8,128)S(1)} custom-call(f32[16,64,128]{2,1,0:T(8,128)S(1)} %all-to-all-done.uv_ref, bf16[2,256,512]{2,1,0:T(8,128)(2,1)S(1)} %copy-done.3, f32[256,128]{1,0:T(8,128)S(1)} %copy-done.7), custom_call_target="tpu_custom_call" | custom-call | tf_op jit(solution)/shard_map/pallas_call | solution.py:388
  35.0 0.8 copy-done.4
  35.8 2.0 %broadcast_multiply_fusion.wall_ref = f32[16,64,128]{2,1,0:T(8,128)} fusion(f32[16,64,128]{2,1,0:T(8,128)} %collective-permute-done, f32[]{:T(128)S(6)} %mul.23), kind=kLoop, calls=%fused_computation | loop fusion | flops 131072 | bytes 1048580 | tf_op jit(solution)/shard_map/mul | solution.py:462
  37.8 14.5 %all-to-all-done.1.rest_ref = f32[16,96,128]{2,1,0:T(8,128)S(1)} async-done(((f32[16,96,128]{2,1,0:T(8,128)}), f32[16,96,128]{2,1,0:T(8,128)S(1)}, u32[]{:S(2)}, u32[]{:S(2)}) %all-to-all-start.1) | async-done | bytes 786464 | tf_op jit(solution)/shard_map/all_to_all | solution.py:413
  52.3 1.0 %copy-done.5 = f32[256,512]{1,0:T(8,128)S(1)} copy-done((f32[256,512]{1,0:T(8,128)S(1)}, f32[256,512]{1,0:T(8,128)}, u32[]{:S(2)}) %copy-start.5) | copy-done | bytes 524312
  53.3 1.0 %copy-done.6 = f32[16,64,128]{2,1,0:T(8,128)S(1)} copy-done((f32[16,64,128]{2,1,0:T(8,128)S(1)}, f32[16,64,128]{2,1,0:T(8,128)}, u32[]{:S(2)}) %copy-start.6) | copy-done | bytes 524312
  54.3 3.7 %shard_map.107 = (f32[16,32,128]{2,1,0:T(8,128)S(1)}, bf16[256,512]{1,0:T(8,128)(2,1)S(1)}, bf16[256,512]{1,0:T(8,128)(2,1)S(1)}) custom-call(f32[16,64,128]{2,1,0:T(8,128)S(1)} %all-to-all-done.uv_ref, f32[16,64,128]{2,1,0:T(8,128)S(1)} %copy-done.6, f32[16,96,128]{2,1,0:T(8,128)S(1)} %all-to-all-done.1.rest_ref, f32[256,512]{1,0:T(8,128)S(1)} %copy-done.5, ...), custom_call_target="tpu_custom_call" | custom-call | tf_op jit(solution)/shard_map/pallas_call | solution.py:388
  60.2 5.1 %all-to-all-start.3 = ((f32[16,32,128]{2,1,0:T(8,128)}), f32[16,32,128]{2,1,0:T(8,128)S(1)}, u32[]{:S(2)}, u32[]{:S(2)}) async-start(f32[16,32,128]{2,1,0:T(8,128)} %copy-done.14), calls=%async_computation.3 | async-start | bytes 524288 | tf_op jit(solution)/shard_map/all_to_all | solution.py:413
  65.4 0.9 %copy-done.18 = bf16[256,512]{1,0:T(8,128)(2,1)S(1)} copy-done((bf16[256,512]{1,0:T(8,128)(2,1)S(1)}, bf16[256,512]{1,0:T(8,128)(2,1)}, u32[]{:S(2)}) %copy-start.18) | copy-done | bytes 262168
  66.3 1.5 %shard_map.108 = f32[16,64,128]{2,1,0:T(8,128)} custom-call(bf16[256,512]{1,0:T(8,128)(2,1)S(1)} %copy-done.16, bf16[256,512]{1,0:T(8,128)(2,1)S(1)} %copy-done.18, bf16[2,512,256]{2,1,0:T(8,128)(2,1)S(1)} %copy-done.2, f32[256,128]{1,0:T(8,128)S(1)} %copy-done.7), custom_call_target="tpu_custom_call" | custom-call | tf_op jit(solution)/shard_map/pallas_call | solution.py:388
  67.8 5.9 %all-to-all-done.3.recv_ref = f32[16,32,128]{2,1,0:T(8,128)S(1)} async-done(((f32[16,32,128]{2,1,0:T(8,128)}), f32[16,32,128]{2,1,0:T(8,128)S(1)}, u32[]{:S(2)}, u32[]{:S(2)}) %all-to-all-start.3) | async-done | bytes 262176 | tf_op jit(solution)/shard_map/all_to_all | solution.py:413
  73.8 3.8 %all-to-all-start.2 = ((f32[16,64,128]{2,1,0:T(8,128)}), f32[16,64,128]{2,1,0:T(8,128)S(1)}, u32[]{:S(2)}, u32[]{:S(2)}) async-start(f32[16,64,128]{2,1,0:T(8,128)} %shard_map.108), calls=%async_computation.2 | async-start | bytes 1048576 | tf_op jit(solution)/shard_map/all_to_all | solution.py:413
  77.7 0.8 shard_map.109.w_ref
  78.6 1.5 %collective-permute-done.2.across_ref = f32[2,32,1024]{2,1,0:T(8,128)S(1)} collective-permute-done((f32[2,32,1024]{2,1,0:T(8,128)S(1)}, f32[2,32,1024]{2,1,0:T(8,128)S(1)}, u32[]{:S(2)}, u32[]{:S(2)}) %collective-permute-start.2) | collective-permute-done | bytes 262176 | tf_op jit(solution)/shard_map/ppermute | solution.py:379
  80.1 11.8 %all-to-all-done.2.recv_ref = f32[16,64,128]{2,1,0:T(8,128)S(1)} async-done(((f32[16,64,128]{2,1,0:T(8,128)}), f32[16,64,128]{2,1,0:T(8,128)S(1)}, u32[]{:S(2)}, u32[]{:S(2)}) %all-to-all-start.2) | async-done | bytes 524320 | tf_op jit(solution)/shard_map/all_to_all | solution.py:413
  91.9 1.9 %shard_map.110 = (f32[3,2,32,1024]{3,2,1,0:T(8,128)}, f32[2,32,1024]{2,1,0:T(8,128)}) custom-call(f32[16,64,128]{2,1,0:T(8,128)S(1)} %all-to-all-done.2.recv_ref, f32[3,2,32,1024]{3,2,1,0:T(8,128)S(1)} %bitcast.9, f32[3,2,32,1024]{3,2,1,0:T(8,128)S(1)} %collective-permute-done.1.side_ref, s32[32,1024]{1,0:T(8,128)S(1)} %copy-done.13, ...), custom_call_target="tpu_custom_call" | custom-call | tf_op jit(solution)/shard_map/pallas_call | solution.py:388
  (41 shorter events, 3.1 us)
Async XLA Ops:
  1.3 1.1 %copy-start = (f32[3,1,2,32,1024]{4,3,2,1,0:T(8,128)S(1)}, f32[3,1,2,32,1024]{4,3,2,1,0:T(8,128)}, u32[]{:S(2)}) copy-start(f32[3,1,2,32,1024]{4,3,2,1,0:T(8,128)} %param.9) | copy-start | bytes 2359300
  2.5 0.9 %copy-start.9 = (bf16[2,256,256]{2,1,0:T(8,128)(2,1)S(1)}, bf16[2,256,256]{2,1,0:T(8,128)(2,1)}, u32[]{:S(2)}) copy-start(bf16[2,256,256]{2,1,0:T(8,128)(2,1)} %constant.37.clone.mat_ref) | copy-start | bytes 786436
  3.4 0.8 copy-start.11
  4.2 10.1 %copy-start.12 = (f32[8,1024]{1,0:T(8,128)S(1)}, f32[8,1024]{1,0:T(8,128)}, u32[]{:S(2)}) copy-start(f32[8,1024]{1,0:T(8,128)} %constant.35.clone.wave_ref) | copy-start | bytes 98308
  5.8 8.5 %copy-start.1 = (f32[3,1,2,32,1024]{4,3,2,1,0:T(8,128)S(1)}, f32[3,1,2,32,1024]{4,3,2,1,0:T(8,128)}, u32[]{:S(2)}) copy-start(f32[3,1,2,32,1024]{4,3,2,1,0:T(8,128)} %param.9) | copy-start | bytes 2359300
  5.8 8.5 %copy-start.10 = (bf16[2,256,256]{2,1,0:T(8,128)(2,1)S(1)}, bf16[2,256,256]{2,1,0:T(8,128)(2,1)}, u32[]{:S(2)}) copy-start(bf16[2,256,256]{2,1,0:T(8,128)(2,1)} %constant.37.clone.mat_ref) | copy-start | bytes 786436
  5.8 23.6 %all-to-all-start = ((f32[16,64,128]{2,1,0:T(8,128)}), f32[16,64,128]{2,1,0:T(8,128)S(1)}, u32[]{:S(2)}, u32[]{:S(2)}) async-start(f32[16,64,128]{2,1,0:T(8,128)} %shard_map.104), calls=%async_computation | async-start | bytes 1048576 | tf_op jit(solution)/shard_map/all_to_all | solution.py:413
  16.0 17.4 %copy-start.3 = (bf16[2,256,512]{2,1,0:T(8,128)(2,1)S(1)}, bf16[2,256,512]{2,1,0:T(8,128)(2,1)}, u32[]{:S(2)}) copy-start(bf16[2,256,512]{2,1,0:T(8,128)(2,1)} %constant.38.clone.to_ref) | copy-start | bytes 1572868
  16.0 17.4 %copy-start.7 = (f32[256,128]{1,0:T(8,128)S(1)}, f32[256,128]{1,0:T(8,128)}, u32[]{:S(2)}) copy-start(f32[256,128]{1,0:T(8,128)} %constant.39.clone.column_ref) | copy-start | bytes 393220
  29.3 22.9 %all-to-all-start.1 = ((f32[16,96,128]{2,1,0:T(8,128)}), f32[16,96,128]{2,1,0:T(8,128)S(1)}, u32[]{:S(2)}, u32[]{:S(2)}) async-start(f32[16,96,128]{2,1,0:T(8,128)} %shard_map.105), calls=%async_computation.1 | async-start | bytes 1572864 | tf_op jit(solution)/shard_map/all_to_all | solution.py:413
  33.3 2.5 %collective-permute-start = (f32[16,64,128]{2,1,0:T(8,128)S(1)}, f32[16,64,128]{2,1,0:T(8,128)}, u32[]{:S(2)}, u32[]{:S(2)}) collective-permute-start(f32[16,64,128]{2,1,0:T(8,128)S(1)} %all-to-all-done.uv_ref), channel_id=1, source_target_pairs={{0,16},{16,0},{1,17},{17,1},{2,18},{18,2},{3,19},{19,3},{4,20},{20... | collective-permute-start | bytes 1572872 | tf_op jit(solution)/shard_map/ppermute | solution.py:379
  35.0 0.8 copy-start.4
  35.8 16.4 %copy-start.2 = (bf16[2,512,256]{2,1,0:T(8,128)(2,1)S(1)}, bf16[2,512,256]{2,1,0:T(8,128)(2,1)}, u32[]{:S(2)}) copy-start(bf16[2,512,256]{2,1,0:T(8,128)(2,1)} %constant.40.clone.from_ref) | copy-start | bytes 1572868
  52.3 1.0 %copy-start.5 = (f32[256,512]{1,0:T(8,128)S(1)}, f32[256,512]{1,0:T(8,128)}, u32[]{:S(2)}) copy-start(f32[256,512]{1,0:T(8,128)} %copy-done.4) | copy-start | bytes 1572868
  53.3 1.0 %copy-start.6 = (f32[16,64,128]{2,1,0:T(8,128)S(1)}, f32[16,64,128]{2,1,0:T(8,128)}, u32[]{:S(2)}) copy-start(f32[16,64,128]{2,1,0:T(8,128)} %broadcast_multiply_fusion.wall_ref) | copy-start | bytes 1572868
  59.5 0.7 copy-start.17
  60.2 5.2 %copy-start.16 = (bf16[256,512]{1,0:T(8,128)(2,1)S(1)}, bf16[256,512]{1,0:T(8,128)(2,1)}, u32[]{:S(2)}) copy-start(bf16[256,512]{1,0:T(8,128)(2,1)} %copy-done.15) | copy-start | bytes 786436
  60.2 13.6 %all-to-all-start.3 = ((f32[16,32,128]{2,1,0:T(8,128)}), f32[16,32,128]{2,1,0:T(8,128)S(1)}, u32[]{:S(2)}, u32[]{:S(2)}) async-start(f32[16,32,128]{2,1,0:T(8,128)} %copy-done.14), calls=%async_computation.3 | async-start | bytes 524288 | tf_op jit(solution)/shard_map/all_to_all | solution.py:413
  65.2 12.4 %collective-permute-start.1 = (f32[3,2,32,1024]{3,2,1,0:T(8,128)S(1)}, f32[3,2,32,1024]{3,2,1,0:T(8,128)S(1)}, u32[]{:S(2)}, u32[]{:S(2)}) collective-permute-start(f32[3,2,32,1024]{3,2,1,0:T(8,128)S(1)} %bitcast.7), channel_id=1, source_target_pairs={{0,16},{16,0},{1,17},{17,1},{2,18},{18,2},{3,19},{19,3},{4,20},{20... | collective-permute-start | bytes 2359304 | tf_op jit(solution)/shard_map/ppermute | solution.py:379
  65.3 1.0 %copy-start.18 = (bf16[256,512]{1,0:T(8,128)(2,1)S(1)}, bf16[256,512]{1,0:T(8,128)(2,1)}, u32[]{:S(2)}) copy-start(bf16[256,512]{1,0:T(8,128)(2,1)} %copy-done.17) | copy-start | bytes 786436
  67.8 9.9 %copy-start.8 = (bf16[2,256,256]{2,1,0:T(8,128)(2,1)S(1)}, bf16[2,256,256]{2,1,0:T(8,128)(2,1)}, u32[]{:S(2)}) copy-start(bf16[2,256,256]{2,1,0:T(8,128)(2,1)} %constant.41.clone.mat_ref) | copy-start | bytes 786436
  67.8 9.9 %copy-start.13 = (s32[32,1024]{1,0:T(8,128)S(1)}, s32[32,1024]{1,0:T(8,128)}, u32[]{:S(2)}) copy-start(s32[32,1024]{1,0:T(8,128)} %mask_ref.3) | copy-start | bytes 393220
  73.8 18.1 %all-to-all-start.2 = ((f32[16,64,128]{2,1,0:T(8,128)}), f32[16,64,128]{2,1,0:T(8,128)S(1)}, u32[]{:S(2)}, u32[]{:S(2)}) async-start(f32[16,64,128]{2,1,0:T(8,128)} %shard_map.108), calls=%async_computation.2 | async-start | bytes 1048576 | tf_op jit(solution)/shard_map/all_to_all | solution.py:413
  78.5 1.6 %collective-permute-start.2 = (f32[2,32,1024]{2,1,0:T(8,128)S(1)}, f32[2,32,1024]{2,1,0:T(8,128)S(1)}, u32[]{:S(2)}, u32[]{:S(2)}) collective-permute-start(f32[2,32,1024]{2,1,0:T(8,128)S(1)} %shard_map.109.w_ref), channel_id=1, source_target_pairs={{0,16},{16,0},{1,17},{17,1},{2,18},{18,2},{3,19},{19,3},{4,20},{20... | collective-permute-start | bytes 786440 | tf_op jit(solution)/shard_map/ppermute | solution.py:379
  (3 other events, 2.1 us)
